TPU v7x, 32 devices: a whole 2x2x4 slice. The times are simulated.
32 devices in a mesh: section: 4 (over y, core), dp: 8 (over z, x).
Axes of the slice: x: 2, y: 2, z: 4, core: 2. Of those that a mesh axis runs over, the one named last changes fastest.
Arguments:
- tokens: bfloat16 [64, 6144], P('dp', 'section'), may hold values from -6 to 6
- expert_ids: int32 [64, 2], P('dp'), may hold values from 0 to 7, all different within a row; in each aligned block of 8 rows (0 to 7, 8 to 15, ...) at most 4 rows name the same one
- router: bfloat16 [6144, 8], replicated, may hold values from -0.078125 to 0.078125
- w_up: bfloat16 [8, 6144, 16384], P('dp', None, 'section'), may hold values from -0.078125 to 0.078125
- w_down: bfloat16 [8, 16384, 6144], P('dp', 'section'), may hold values from -0.0625 to 0.0625
- attn_queries: bfloat16 [8, 128, 6144], P('dp', None, 'section'), may hold values from -140 to 140
- attn_keys: bfloat16 [8, 128, 6144], P('dp', None, 'section'), may hold values from -8 to 8
- attn_values: bfloat16 [8, 128, 6144], P('dp', None, 'section'), may hold values from -6 to 6
Outputs:
- mixed: bfloat16 [64, 6144], P('dp', 'section')
- attended: bfloat16 [8, 128, 6144], P('dp', None, 'section')
Inputs may be any that keep to these rules, and one draw needn't show every extreme that they name: `expert_ids`: each row names two different experts; among the 8 rows of one dp index (aligned blocks) no expert is named more than 4 times.
All inputs are finite; a program needn't handle non-finite values.
Results may differ from a plain program's by a relative error of at most 0.005.
Values may be sent and summed in bfloat16 or wider, within the bound.
A program may use at most 192 MiB of HBM per device.

v0:
```python
import functools
import math

import jax
import jax.numpy as jnp
from jax import lax
from jax.experimental import pallas as pl
from jax.experimental.pallas import tpu as pltpu
from jax.sharding import PartitionSpec as P

HEAD_DIM = 128
MESH = pl.DeviceIdType.MESH


def aligned(index, size):
    return pl.ds(pl.multiple_of(index * size, size), size)


def kernel(
    dims,
    tokens_hbm,
    ids_hbm,
    router_hbm,
    up_hbm,
    down_hbm,
    q_hbm,
    k_hbm,
    v_hbm,
    mixed_hbm,
    attended_hbm,
    ring,
    x_all,
    x_rows,
    hidden,
    stage,
    terms,
    returning,
    received,
    router,
    ids,
    logits,
    q,
    k,
    v,
    attended,
    mixed,
    small_sem,
    up_sem,
    down_sem,
    send_sem,
    line_sem,
    plane_sem,
    x_sem,
    term_sem,
    back_sem,
    part_sem,
    own_sem,
    out_sem,
):
    n_sec, n_dp, rows, cols, experts = dims
    per_block, width = tokens_hbm.shape
    model, ff = up_hbm.shape[1:]
    devices = n_sec * n_dp
    up_blocks, up_units = ff // cols, model // rows
    down_blocks, down_units = model // cols, ff // rows
    sec_blocks = width // cols
    s, g = lax.axis_index("section"), lax.axis_index("dp")
    me = s * n_dp + g
    half, lines = n_sec // 2, n_dp // 2
    y, core, line, x = s // 2, s % 2, g // 2, g % 2

    def slot(y_at, core_at, dp):
        return (core_at * half + y_at) * n_dp + dp

    mine = slot(y, core, g)

    copies = [
        pltpu.make_async_copy(tokens_hbm, x_all.at[mine], small_sem.at[0]),
        pltpu.make_async_copy(q_hbm.at[0], q, small_sem.at[1]),
        pltpu.make_async_copy(k_hbm.at[0], k, small_sem.at[2]),
        pltpu.make_async_copy(v_hbm.at[0], v, small_sem.at[3]),
        pltpu.make_async_copy(router_hbm, router, small_sem.at[4]),
        pltpu.make_async_copy(ids_hbm, ids, small_sem.at[5]),
    ]
    for copy in copies:
        copy.start()

    def up_copy(n):
        return pltpu.make_async_copy(
            up_hbm.at[0, :, aligned(n, cols)], ring.at[aligned(n, model)], up_sem.at[n]
        )

    @pl.loop(0, up_blocks)
    def _(n):
        up_copy(n).start()

    barrier = pltpu.get_barrier_semaphore()

    def place(index):
        return {"section": index // n_dp, "dp": index % n_dp}

    @pl.loop(1, devices)
    def _(offset):
        peer = (me + offset) % devices
        pl.semaphore_signal(barrier, inc=1, device_id=place(peer), device_id_type=MESH)

    for copy in copies[1:4]:
        copy.wait()
    length = q.shape[0]
    heads = width // HEAD_DIM
    group = math.gcd(heads, 4)
    causal = lax.broadcasted_iota(jnp.int32, (length, length), 1) <= lax.broadcasted_iota(
        jnp.int32, (length, length), 0
    )

    def attend(third):
        steps = heads // group
        pl.loop(steps * third // 3, steps * (third + 1) // 3)(attend_heads)

    def attend_heads(step):
        for lane in range(group):
            at = aligned(step * group + lane, HEAD_DIM)
            scores = lax.dot_general(
                q[:, at], k[:, at], (((1,), (1,)), ((), ())), preferred_element_type=jnp.float32
            ) * (1.0 / math.sqrt(HEAD_DIM))
            scores = jnp.where(causal, scores, -jnp.inf)
            exps = jnp.exp(scores - jnp.max(scores, axis=1, keepdims=True))
            probs = (exps / jnp.sum(exps, axis=1, keepdims=True)).astype(jnp.bfloat16)
            attended[:, at] = jnp.dot(
                probs, v[:, at], preferred_element_type=jnp.float32
            ).astype(jnp.bfloat16)

    attend(0)
    copies[0].wait()
    pl.semaphore_wait(barrier, devices - 1)

    def send_tokens(block, sem, place):
        pltpu.make_async_remote_copy(
            src_ref=x_all.at[block],
            dst_ref=x_all.at[block],
            send_sem=send_sem,
            recv_sem=sem,
            device_id=place,
            device_id_type=MESH,
        ).start()

    @pl.loop(1, lines)
    def _(offset):
        to = (line + offset) % lines
        send_tokens(mine, line_sem.at[offset], {"section": s, "dp": to * 2 + x})

    def spread(from_line):
        block = slot(y, core, from_line * 2 + x)

        @pl.loop(1, 2 * half)
        def _(offset):
            to_y, to_x = (y + offset // 2) % half, (x + offset) % 2
            send_tokens(
                block, plane_sem, {"section": to_y * 2 + core, "dp": line * 2 + to_x}
            )

    spread(line)
    attend(1)

    @pl.loop(1, lines)
    def _(offset):
        from_line = (line + lines - offset) % lines
        block = x_all.at[slot(y, core, from_line * 2 + x)]
        pltpu.make_async_copy(block, block, line_sem.at[offset]).wait()
        spread(from_line)

    n_half = half * n_dp
    plane = x_all.at[pl.ds(0, n_half - lines)]
    pltpu.make_async_copy(plane, plane, plane_sem).wait()
    send_tokens(pl.ds(core * n_half, n_half), x_sem, {"section": y * 2 + 1 - core, "dp": g})

    attend(2)
    attended_copy = pltpu.make_async_copy(attended, attended_hbm.at[0], out_sem.at[0])
    attended_copy.start()

    others = x_all.at[pl.ds(0, devices - 1)]
    arrived = x_all.at[pl.ds(0, n_half)]
    pltpu.make_async_copy(arrived, arrived, x_sem).wait()
    for part in range(n_sec):
        at = pl.ds((part % half * 2 + part // half) * width, width)
        for pair in range(n_dp // 2):
            first = x_all[part * n_dp + 2 * pair].astype(jnp.float32)
            second = x_all[part * n_dp + 2 * pair + 1].astype(jnp.float32)
            x_rows[pl.ds(2 * pair * per_block, 2 * per_block), at] = jnp.concatenate(
                [first, second], axis=0
            ).astype(jnp.bfloat16)

    def down_place(block):
        turn = block // sec_blocks
        to_y, to_core = (y + 1 + turn // 2) % half, (core + 1 + turn) % 2
        return to_y * 2 + to_core, block % sec_blocks

    def down_copy(unit):
        block, part = unit // down_units, unit % down_units
        sec, col = down_place(block)
        return pltpu.make_async_copy(
            down_hbm.at[0, aligned(part, rows), aligned(sec * sec_blocks + col, cols)],
            ring.at[aligned(unit, rows)],
            down_sem.at[block],
        )

    @pl.loop(0, up_blocks)
    def _(n):
        up_copy(n).wait()
        value = jnp.dot(
            x_rows[...], ring[aligned(n, model), :], preferred_element_type=jnp.float32
        )
        hidden[:, aligned(n, cols)] = (value / (1.0 + jnp.exp(-value))).astype(jnp.bfloat16)
        for unit in range(up_units):
            down_copy(n * up_units + unit).start()

    copies[4].wait()
    copies[5].wait()
    logits[...] = lax.dot_general(
        x_rows[...], router[...], (((1,), (1,)), ((), ())), preferred_element_type=jnp.float32
    )
    own = logits[aligned(g, per_block), :]
    lanes = lax.broadcasted_iota(jnp.int32, (per_block, experts), 1)
    diagonal = lax.broadcasted_iota(jnp.int32, (per_block, per_block), 0) == lax.broadcasted_iota(
        jnp.int32, (per_block, per_block), 1
    )

    def column(which):
        row = jnp.broadcast_to(ids[which : which + 1, :].astype(jnp.float32), diagonal.shape)
        return jnp.sum(jnp.where(diagonal, row, 0.0), axis=1, keepdims=True).astype(jnp.int32)

    is_first, is_second = column(0) == lanes, column(1) == lanes
    gap = jnp.sum(jnp.where(is_first, own, 0.0), axis=1, keepdims=True) - jnp.sum(
        jnp.where(is_second, own, 0.0), axis=1, keepdims=True
    )
    first_prob = 1.0 / (1.0 + jnp.exp(-gap))
    coefficient = jnp.where(is_first, first_prob, 0.0) + jnp.where(
        is_second, 1.0 - first_prob, 0.0
    )

    def down_block(block):
        taken = ring.at[aligned(block, ff)]
        pltpu.make_async_copy(taken, taken, down_sem.at[block]).wait()
        return jnp.dot(hidden[...], taken[...], preferred_element_type=jnp.float32)

    away = (n_sec - 1) * sec_blocks

    @pl.loop(0, away)
    def _(block):
        stage[block] = down_block(block).astype(jnp.bfloat16)
        sec, col = down_place(block)
        pltpu.make_async_remote_copy(
            src_ref=stage.at[block],
            dst_ref=terms.at[block // sec_blocks, :, aligned(col, cols)],
            send_sem=term_sem.at[0],
            recv_sem=term_sem.at[1],
            device_id={"section": sec, "dp": g},
            device_id_type=MESH,
        ).start()

    pltpu.make_async_copy(terms, terms, term_sem.at[1]).wait()

    @pl.loop(away, down_blocks)
    def _(block):
        at = aligned(block - away, cols)
        summed = down_block(block)
        for term in range(n_sec - 1):
            summed += terms[term, :, at].astype(jnp.float32)
        for b in range(n_dp):
            returning[block - away, b] = summed[b * per_block : (b + 1) * per_block].astype(
                jnp.bfloat16
            )

        @pl.loop(1, n_dp)
        def _(offset):
            b = (g + offset) % n_dp
            pltpu.make_async_remote_copy(
                src_ref=returning.at[block - away, b],
                dst_ref=received.at[g, :, at],
                send_sem=part_sem,
                recv_sem=back_sem,
                device_id={"section": s, "dp": b},
                device_id_type=MESH,
            ).start()

        pltpu.make_async_copy(
            returning.at[block - away, g], received.at[g, :, at], own_sem
        ).start()

    own_row = received.at[g]
    pltpu.make_async_copy(own_row, own_row, own_sem).wait()
    rest = received.at[pl.ds(0, n_dp - 1)]
    pltpu.make_async_copy(rest, rest, back_sem).wait()

    shares = [
        jnp.broadcast_to(coefficient[:, e : e + 1], (per_block, width)) for e in range(experts)
    ]
    per_expert = n_dp // experts

    total = jnp.zeros((per_block, width), jnp.float32)
    for b in range(n_dp):
        total += shares[b // per_expert] * received[b].astype(jnp.float32)
    mixed[...] = total.astype(jnp.bfloat16)
    mixed_copy = pltpu.make_async_copy(mixed, mixed_hbm, out_sem.at[1])
    mixed_copy.start()

    pltpu.make_async_copy(others, others, send_sem).wait()
    pltpu.make_async_copy(rest, rest, part_sem).wait()
    pltpu.make_async_copy(terms, terms, term_sem.at[0]).wait()
    attended_copy.wait()
    mixed_copy.wait()


def per_device(tokens, expert_ids, router, w_up, w_down, attn_queries, attn_keys, attn_values):
    n_sec, n_dp = lax.axis_size("section"), lax.axis_size("dp")
    per_block, width = tokens.shape
    model, experts = router.shape
    ff = w_up.shape[2]
    length = attn_queries.shape[1]
    devices = n_sec * n_dp
    rows, cols = math.gcd(model, ff), math.gcd(ff, width)
    down_blocks = model // cols
    bf16, f32 = jnp.bfloat16, jnp.float32
    any_spec = pl.BlockSpec(memory_space=pl.ANY)
    return pl.pallas_call(
        functools.partial(kernel, (n_sec, n_dp, rows, cols, experts)),
        out_shape=(
            jax.ShapeDtypeStruct(tokens.shape, bf16),
            jax.ShapeDtypeStruct(attn_queries.shape, bf16),
        ),
        in_specs=[any_spec] * 8,
        out_specs=(any_spec, any_spec),
        scratch_shapes=[
            pltpu.VMEM((model * ff // cols, cols), bf16),
            pltpu.VMEM((devices, per_block, width), bf16),
            pltpu.VMEM((n_dp * per_block, model), bf16),
            pltpu.VMEM((n_dp * per_block, ff), bf16),
            pltpu.VMEM((down_blocks - width // cols, n_dp * per_block, cols), bf16),
            pltpu.VMEM((n_sec - 1, n_dp * per_block, width), bf16),
            pltpu.VMEM((width // cols, n_dp, per_block, cols), bf16),
            pltpu.VMEM((n_dp, per_block, width), bf16),
            pltpu.VMEM((experts, model), bf16),
            pltpu.VMEM((2, per_block), jnp.int32),
            pltpu.VMEM((n_dp * per_block, experts), f32),
            pltpu.VMEM((length, width), bf16),
            pltpu.VMEM((length, width), bf16),
            pltpu.VMEM((length, width), bf16),
            pltpu.VMEM((length, width), bf16),
            pltpu.VMEM((per_block, width), bf16),
            pltpu.SemaphoreType.DMA((6,)),
            pltpu.SemaphoreType.DMA((ff // cols,)),
            pltpu.SemaphoreType.DMA((down_blocks,)),
            pltpu.SemaphoreType.DMA,
            pltpu.SemaphoreType.DMA((n_dp // 2,)),
            pltpu.SemaphoreType.DMA,
            pltpu.SemaphoreType.DMA,
            pltpu.SemaphoreType.DMA((2,)),
            pltpu.SemaphoreType.DMA,
            pltpu.SemaphoreType.DMA,
            pltpu.SemaphoreType.DMA,
            pltpu.SemaphoreType.DMA((2,)),
        ],
        compiler_params=pltpu.CompilerParams(
            collective_id=0, has_side_effects=True, vmem_limit_bytes=67043328
        ),
    )(tokens, expert_ids.T, router.T, w_up, w_down, attn_queries, attn_keys, attn_values)


def solution(mesh):
    placed = (
        P("dp", "section"),
        P("dp", None),
        P(),
        P("dp", None, "section"),
        P("dp", "section", None),
        P("dp", None, "section"),
        P("dp", None, "section"),
        P("dp", None, "section"),
    )
    return jax.shard_map(
        per_device,
        mesh=mesh,
        in_specs=placed,
        out_specs=(P("dp", "section"), P("dp", None, "section")),
        check_vma=False,
    )
```

profile of v0, /device:TPU:0, one launch (start us, length us, event | category | flops | bytes accessed | tf_op | source)
XLA Modules:
  0.0 50.9 jit_solution(5821723256393472411)
XLA Ops:
  0.6 47.1 %shard_map.95 = (bf16[8,1536]{1,0:T(8,128)(2,1)}, bf16[1,128,1536]{2,1,0:T(8,128)(2,1)}) custom-call(bf16[8,1536]{1,0:T(8,128)(2,1)} %tokens_hbm.1, s32[2,8]{1,0:T(2,128)} %bitcast.3, bf16[8,6144]{1,0:T(8,128)(2,1)} %bitcast.2, bf16[1,6144,4096]{2,1,0:T(8,128)(2,1)} %up_hbm.1, bf16[1,4096,6144]{2,1,0:T(8,128)(2,1)} %down_hbm.1, bf16[1,128,1536]{2,1,0:T(8,128)(2,1)} %q_hbm.1, ...), custom_call_target="tpu_custom_call" | custom-call | tf_op jit(solution)/shard_map/pallas_call | solution.py:325
  47.8 1.3 %copy.12 = bf16[8,1536]{1,0:T(8,128)(2,1)} copy(bf16[8,1536]{1,0:T(8,128)(2,1)} %get-tuple-element.4) | data formatting | bytes 49152
  49.1 1.8 %copy.13 = bf16[1,128,1536]{2,1,0:T(8,128)(2,1)} copy(bf16[1,128,1536]{2,1,0:T(8,128)(2,1)} %get-tuple-element.5) | data formatting | bytes 786432
where the time goes:
time: 51.1 us; the launch traced here: 50.9 us
  Pallas kernels  47.1 us (92%)
  local copies, waits for them, and re-layouts  3.11 us (6%)
  between operations  0.64 us (1%)
    pallas_call x1, Pallas kernels, per_device(): pl.pallas_call(functools.partial(kernel, (n_sec, n_dp, rows, cols, expert...  47.1 us
    unnamed x2, local copies, waits for them, and re-layouts  3.11 us

commit v1 on v0

v1 whole, which is shorter than its diff:
```python
import functools
import math

import jax
import jax.numpy as jnp
from jax import lax
from jax.experimental import pallas as pl
from jax.experimental.pallas import tpu as pltpu
from jax.sharding import PartitionSpec as P

HEAD_DIM = 128
LANES = 128
CAP = 4
MESH = pl.DeviceIdType.MESH


def aligned(index, size):
    return pl.ds(pl.multiple_of(index * size, size), size)


def kernel(
    dims,
    tokens_hbm,
    ids_hbm,
    router_hbm,
    up_hbm,
    down_hbm,
    q_hbm,
    k_hbm,
    v_hbm,
    mixed,
    attended,
    ring,
    tokens,
    outgoing,
    planes,
    x_rows,
    acc,
    hidden,
    stage,
    terms,
    returning,
    received,
    router,
    ids,
    logit_terms,
    coefficient,
    q,
    k,
    v,
    small_sem,
    up_sem,
    down_sem,
    send_sem,
    plane_sem,
    y_sem,
    pair_sem,
    logit_sem,
    term_sem,
    back_sem,
):
    n_sec, n_dp, cols, experts, fold, up_group, rows = dims
    per_block, width = tokens.shape
    ff = down_hbm.shape[1]
    slots, wide, part = per_block // fold, width // fold, cols // fold
    up_blocks, sec_blocks = ff // cols, width // cols
    groups, freed = up_blocks // up_group, up_group * width // rows
    down_units = ff // rows
    per_expert = n_dp // experts
    away = (n_sec - 1) * sec_blocks
    bf16, f32 = jnp.bfloat16, jnp.float32
    s, g = lax.axis_index("section"), lax.axis_index("dp")
    half = n_sec // 2
    y, core = s // 2, s % 2
    partner = {"section": y * 2 + 1 - core, "dp": g}

    def copy_in(index, source, target):
        return pltpu.make_async_copy(source, target, small_sem.at[index])

    copies = [
        copy_in(0, ids_hbm, ids),
        copy_in(1, tokens_hbm, tokens),
        copy_in(2, router_hbm.at[:, aligned(s, width)], router),
        copy_in(3, q_hbm.at[0], q),
        copy_in(4, k_hbm.at[0], k),
        copy_in(5, v_hbm.at[0], v),
    ]
    for copy in copies:
        copy.start()

    def section_of(j):
        return (y + half - j // 2) % half * 2 + (core + j) % 2

    def up_copy(j, n):
        unit = j * up_blocks + n
        return pltpu.make_async_copy(
            up_hbm.at[0, aligned(section_of(j), width), aligned(n, cols)],
            ring.at[aligned(unit, width)],
            up_sem.at[unit],
        )

    @pl.loop(0, n_sec * up_blocks)
    def _(unit):
        up_copy(unit // up_blocks, unit % up_blocks).start()

    barrier = pltpu.get_barrier_semaphore()

    def greet(place):
        pl.semaphore_signal(barrier, inc=1, device_id=place, device_id_type=MESH)

    @pl.loop(1, n_dp)
    def _(offset):
        greet({"section": s, "dp": (g + offset) % n_dp})

    @pl.loop(1, n_sec)
    def _(offset):
        greet({"section": (s + offset) % n_sec, "dp": g})

    def send(source, target, sems, place):
        pltpu.make_async_remote_copy(
            src_ref=source,
            dst_ref=target,
            send_sem=sems[0],
            recv_sem=sems[1],
            device_id=place,
            device_id_type=MESH,
        ).start()

    def await_bytes(like, sem):
        pltpu.make_async_copy(like, like, sem).wait()

    iota = functools.partial(lax.broadcasted_iota, jnp.int32)
    slot_bits, row_bits = slots.bit_length() - 1, per_block.bit_length() - 1

    def split_rows(index):
        within = index & (per_block - 1)
        return index >> row_bits, within >> slot_bits, within & (slots - 1)

    copies[0].wait()
    shape = (experts * per_block, per_block)
    expert, run, slot = split_rows(iota(shape, 0))
    named = (ids[0:1, :] == expert) | (ids[1:2, :] == expert)
    square = (per_block, per_block)
    earlier = (iota(square, 0) < iota(square, 1)).astype(f32).astype(bf16)
    rank = jnp.dot(named.astype(f32).astype(bf16), earlier, preferred_element_type=f32)
    picked = named & (rank == slot.astype(f32))
    copies[1].wait()
    packed = sum(
        jnp.dot(
            (picked & (run == h)).astype(f32).astype(bf16),
            tokens[:, h * wide : (h + 1) * wide],
            preferred_element_type=f32,
        )
        for h in range(fold)
    )
    for e in range(experts):
        outgoing[e] = packed[e * per_block : (e + 1) * per_block].astype(bf16)
    planes[s, g] = outgoing[g // per_expert]

    pl.semaphore_wait(barrier, n_dp + n_sec - 2)

    @pl.loop(1, n_dp)
    def _(offset):
        to = (g + offset) % n_dp
        send(
            outgoing.at[to // per_expert],
            planes.at[s, g],
            (send_sem.at[0], plane_sem),
            {"section": s, "dp": to},
        )

    copies[2].wait()
    partial = lax.dot_general(
        tokens[...], router[...], (((1,), (1,)), ((), ())), preferred_element_type=f32
    )
    logit_terms[s] = jnp.concatenate(
        [partial, jnp.zeros((per_block, LANES - experts), f32)], axis=1
    )

    @pl.loop(1, n_sec)
    def _(offset):
        send(
            logit_terms.at[s],
            logit_terms.at[s],
            (send_sem.at[2], logit_sem),
            {"section": (s + offset) % n_sec, "dp": g},
        )

    for copy in copies[3:]:
        copy.wait()
    length = q.shape[0]
    heads = width // HEAD_DIM
    together = math.gcd(heads, 4)
    causal = iota((length, length), 1) <= iota((length, length), 0)

    def attend(third):
        steps = heads // together
        pl.loop(steps * third // 3, steps * (third + 1) // 3)(attend_heads)

    def attend_heads(step):
        for lane in range(together):
            at = aligned(step * together + lane, HEAD_DIM)
            scores = lax.dot_general(
                q[:, at], k[:, at], (((1,), (1,)), ((), ())), preferred_element_type=f32
            ) * (1.0 / math.sqrt(HEAD_DIM))
            scores = jnp.where(causal, scores, -jnp.inf)
            exps = jnp.exp(scores - jnp.max(scores, axis=1, keepdims=True))
            probs = (exps / jnp.sum(exps, axis=1, keepdims=True)).astype(bf16)
            attended[0, :, at] = jnp.dot(
                probs, v[:, at], preferred_element_type=f32
            ).astype(bf16)

    attend(0)
    attend(1)

    def down_place(block):
        turn = block // sec_blocks
        to_y, to_core = (y + 1 + turn // 2) % half, (core + 1 + turn) % 2
        return to_y * 2 + to_core, block % sec_blocks

    def down_copy(unit):
        block, piece = unit // down_units, unit % down_units
        sec, col = down_place(block)
        return pltpu.make_async_copy(
            down_hbm.at[0, aligned(piece, rows), aligned(sec * sec_blocks + col, cols)],
            ring.at[aligned(unit, rows)],
            down_sem.at[block],
        )

    low = iota((per_block, 1), 0) < slots

    def exchange(first, second):
        turned = [pltpu.roll(value, slots, 0) for value in (first, second)]
        return jnp.where(low, first, turned[1]), jnp.where(low, turned[0], second)

    def assemble(j, sec):
        @pl.loop(0, n_dp // (2 * fold))
        def _(group):
            held = [
                planes[sec, group * (2 * fold) + b].astype(f32) for b in range(2 * fold)
            ]
            if fold == 2:
                pairs = [exchange(*held[:2]), exchange(*held[2:])]
                runs = [[pair[h] for pair in pairs] for h in range(2)]
            else:
                runs = [held]
            for h, run in enumerate(runs):
                x_rows[j, aligned(group, 2 * per_block), h * wide : (h + 1) * wide] = (
                    jnp.concatenate(run, axis=0).astype(bf16)
                )

    def phase(j, first, last):
        assemble(j, section_of(j))

        @pl.loop(0, groups)
        def _(group):
            for lane in range(up_group):
                up_copy(j, group * up_group + lane).wait()
            for lane in range(up_group):
                n = group * up_group + lane
                at = aligned(n, cols)
                value = jnp.dot(
                    x_rows[j],
                    ring[aligned(j * up_blocks + n, width), :],
                    preferred_element_type=f32,
                )
                if not first:
                    value += acc[:, at]
                if last:
                    hidden[:, at] = (value / (1.0 + jnp.exp(-value))).astype(bf16)
                else:
                    acc[:, at] = value

            @pl.loop(0, freed)
            def _(unit):
                down_copy((j * groups + group) * freed + unit).start()

    await_bytes(planes.at[s, pl.ds(0, n_dp - 1)], plane_sem)

    @pl.loop(1, half)
    def _(t):
        send(
            planes.at[s],
            planes.at[s],
            (send_sem.at[1], y_sem.at[t]),
            {"section": (y + t) % half * 2 + core, "dp": g},
        )

    send(planes.at[s], planes.at[s], (send_sem.at[1], pair_sem.at[0]), partner)
    phase(0, True, False)

    @pl.loop(1, n_sec - 1)
    def _(j):
        sec, t = section_of(j), j // 2

        @pl.when(j % 2 == 0)
        def _():
            await_bytes(planes.at[sec], y_sem.at[t])
            send(planes.at[sec], planes.at[sec], (send_sem.at[1], pair_sem.at[t]), partner)

        @pl.when(j % 2 == 1)
        def _():
            await_bytes(planes.at[sec], pair_sem.at[t])

        phase(j, False, False)

    await_bytes(planes.at[section_of(n_sec - 1)], pair_sem.at[half - 1])
    phase(n_sec - 1, False, True)
    attend(2)

    await_bytes(logit_terms.at[pl.ds(0, n_sec - 1)], logit_sem)
    logits = logit_terms[0]
    for sec in range(1, n_sec):
        logits += logit_terms[sec]
    diagonal = iota(square, 0) == iota(square, 1)

    def column(which):
        row = jnp.broadcast_to(ids[which : which + 1, :].astype(f32), diagonal.shape)
        return jnp.sum(jnp.where(diagonal, row, 0.0), axis=1, keepdims=True).astype(jnp.int32)

    first_id, second_id = column(0), column(1)
    lanes = iota((per_block, LANES), 1)

    def logit(which):
        return jnp.sum(jnp.where(lanes == which, logits, 0.0), axis=1, keepdims=True)

    first_prob = 1.0 / (1.0 + jnp.exp(logit(second_id) - logit(first_id)))
    source, run, slot = split_rows(iota((per_block, n_dp * per_block), 1))
    expert = source >> (per_expert.bit_length() - 1)
    is_first, is_second = first_id == expert, second_id == expert
    named = is_first | is_second
    before = (iota(square, 1) < iota(square, 0)).astype(f32).astype(bf16)
    rank = jnp.dot(before, named.astype(f32).astype(bf16), preferred_element_type=f32)
    weight = jnp.where(is_first, first_prob, 0.0) + jnp.where(is_second, 1.0 - first_prob, 0.0)
    weight = jnp.where(rank == slot.astype(f32), weight, 0.0)
    weights = jnp.concatenate(
        [jnp.where(run == h, weight, 0.0) for h in range(fold)], axis=0
    )
    coarse = weights.astype(bf16).astype(f32)
    coefficient[...] = jnp.concatenate([coarse, weights - coarse], axis=0).astype(bf16)

    def down_block(block):
        taken = ring.at[aligned(block, ff)]
        await_bytes(taken, down_sem.at[block])
        return jnp.dot(hidden[...], taken[...], preferred_element_type=f32)

    @pl.loop(0, away)
    def _(block):
        stage[block] = down_block(block).astype(bf16)
        sec, col = down_place(block)
        send(
            stage.at[block],
            terms.at[block // sec_blocks, :, aligned(col, cols)],
            (send_sem.at[3], term_sem),
            {"section": sec, "dp": g},
        )

    await_bytes(terms, term_sem)

    @pl.loop(0, sec_blocks)
    def _(block):
        summed = down_block(away + block)
        for term in range(n_sec - 1):
            summed += terms[term, :, aligned(block, cols)].astype(f32)
        for b in range(n_dp // fold):
            piece = summed[b * per_block : (b + 1) * per_block]
            if fold == 2:
                back = exchange(piece[:, :part], piece[:, part:])
            else:
                back = [piece]
            for i in range(fold):
                returning[block, b * fold + i] = back[i].astype(bf16)

        @pl.loop(1, n_dp)
        def _(offset):
            b = (g + offset) % n_dp
            send(
                returning.at[block, b],
                received.at[block, g],
                (send_sem.at[4], back_sem.at[block]),
                {"section": s, "dp": b},
            )

        received[block, g] = returning[block, g]

    @pl.loop(0, sec_blocks)
    def _(block):
        await_bytes(received.at[block, pl.ds(0, n_dp - 1)], back_sem.at[block])
        rows_back = jnp.concatenate(
            [received[block, b].astype(f32) for b in range(n_dp)], axis=0
        ).astype(bf16)
        both = jnp.dot(coefficient[...], rows_back, preferred_element_type=f32)
        tall = fold * per_block
        total = both[:tall] + both[tall:]
        for h in range(fold):
            at = pl.ds(pl.multiple_of(block * cols + h * part, part), part)
            mixed[:, at] = total[h * per_block : (h + 1) * per_block].astype(bf16)

    await_bytes(planes.at[0, pl.ds(0, n_dp - 1)], send_sem.at[0])
    await_bytes(planes.at[pl.ds(0, n_sec - 1)], send_sem.at[1])
    await_bytes(logit_terms.at[pl.ds(0, n_sec - 1)], send_sem.at[2])
    await_bytes(terms, send_sem.at[3])
    await_bytes(received.at[:, pl.ds(0, n_dp - 1)], send_sem.at[4])


def write_out(mixed, attended, mixed_hbm, attended_hbm, sems):
    copies = [
        pltpu.make_async_copy(mixed, mixed_hbm, sems.at[0]),
        pltpu.make_async_copy(attended, attended_hbm, sems.at[1]),
    ]
    for copy in copies:
        copy.start()
    for copy in copies:
        copy.wait()


def per_device(tokens, expert_ids, router, w_up, w_down, attn_queries, attn_keys, attn_values):
    n_sec, n_dp = lax.axis_size("section"), lax.axis_size("dp")
    per_block, width = tokens.shape
    model, experts = router.shape
    ff = w_up.shape[2]
    length = attn_queries.shape[1]
    cols = math.gcd(ff, width)
    fold = per_block // CAP if cols % (2 * LANES) == 0 else 1
    up_group = math.gcd(ff // cols, 4)
    rows = math.gcd(up_group * width, ff)
    slots, wide, part = per_block // fold, width // fold, cols // fold
    tall, down_blocks, sec_blocks = n_dp * slots, model // cols, width // cols
    bf16, f32 = jnp.bfloat16, jnp.float32
    any_spec = pl.BlockSpec(memory_space=pl.ANY)
    vmem_spec = pl.BlockSpec(memory_space=pltpu.VMEM)
    shapes = tokens.shape, attn_queries.shape
    held = pl.pallas_call(
        functools.partial(kernel, (n_sec, n_dp, cols, experts, fold, up_group, rows)),
        out_shape=tuple(pltpu.VMEM(shape, bf16) for shape in shapes),
        in_specs=[any_spec] * 8,
        out_specs=(vmem_spec, vmem_spec),
        scratch_shapes=[
            pltpu.VMEM((model * ff // cols, cols), bf16),
            pltpu.VMEM((per_block, width), bf16),
            pltpu.VMEM((experts, per_block, wide), bf16),
            pltpu.VMEM((n_sec, n_dp, per_block, wide), bf16),
            pltpu.VMEM((n_sec, tall, width), bf16),
            pltpu.VMEM((tall, ff), f32),
            pltpu.VMEM((tall, ff), bf16),
            pltpu.VMEM((down_blocks - sec_blocks, tall, cols), bf16),
            pltpu.VMEM((n_sec - 1, tall, width), bf16),
            pltpu.VMEM((sec_blocks, n_dp, per_block, part), bf16),
            pltpu.VMEM((sec_blocks, n_dp, per_block, part), bf16),
            pltpu.VMEM((experts, width), bf16),
            pltpu.VMEM((2, per_block), jnp.int32),
            pltpu.VMEM((n_sec, per_block, LANES), f32),
            pltpu.VMEM((2 * fold * per_block, n_dp * per_block), bf16),
            pltpu.VMEM((length, width), bf16),
            pltpu.VMEM((length, width), bf16),
            pltpu.VMEM((length, width), bf16),
            pltpu.SemaphoreType.DMA((6,)),
            pltpu.SemaphoreType.DMA((n_sec * ff // cols,)),
            pltpu.SemaphoreType.DMA((down_blocks,)),
            pltpu.SemaphoreType.DMA((5,)),
            pltpu.SemaphoreType.DMA,
            pltpu.SemaphoreType.DMA((n_sec // 2,)),
            pltpu.SemaphoreType.DMA((n_sec // 2,)),
            pltpu.SemaphoreType.DMA,
            pltpu.SemaphoreType.DMA,
            pltpu.SemaphoreType.DMA((sec_blocks,)),
        ],
        compiler_params=pltpu.CompilerParams(
            collective_id=0, has_side_effects=True, vmem_limit_bytes=62 * 2**20
        ),
    )(tokens, expert_ids.T, router.T, w_up, w_down, attn_queries, attn_keys, attn_values)
    return pl.pallas_call(
        write_out,
        out_shape=tuple(jax.ShapeDtypeStruct(shape, bf16) for shape in shapes),
        in_specs=[vmem_spec, vmem_spec],
        out_specs=(any_spec, any_spec),
        scratch_shapes=[pltpu.SemaphoreType.DMA((2,))],
    )(*(pltpu.with_memory_space_constraint(value, pltpu.VMEM) for value in held))


def solution(mesh):
    placed = (
        P("dp", "section"),
        P("dp", None),
        P(),
        P("dp", None, "section"),
        P("dp", "section", None),
        P("dp", None, "section"),
        P("dp", None, "section"),
        P("dp", None, "section"),
    )
    return jax.shard_map(
        per_device,
        mesh=mesh,
        in_specs=placed,
        out_specs=(P("dp", "section"), P("dp", None, "section")),
        check_vma=False,
    )
```

time: 51.1 us -> 41.8 us (0.82)
  Pallas kernels: 47.1 us -> 41 us
  local copies, waits for them, and re-layouts: 3.11 us -> 0 us
    pallas_call x1 -> x2, Pallas kernels: 47.1 us -> 41 us  [the longest x1 40.3 us: per_device(): pl.pallas_call(functools.partial(kernel, (n_sec, n_dp, cols, experts, fol...]
    unnamed x2 -> x0, local copies, waits for them, and re-layouts: 3.11 us -> none
where the time goes in v1:
time: 41.8 us; the launch traced here: 41.7 us
  Pallas kernels  41 us (98%)
  between operations  0.64 us (2%)
    pallas_call x1, Pallas kernels, per_device(): pl.pallas_call(functools.partial(kernel, (n_sec, n_dp, cols, experts, fol...  40.3 us

profile of v1, /device:TPU:0, one launch (start us, length us, event | category | flops | bytes accessed | tf_op | source)
XLA Modules:
  0.0 41.7 jit_solution(18175373671163999826)
XLA Ops:
  0.6 40.3 %shard_map.95 = (bf16[8,1536]{1,0:T(8,128)(2,1)S(1)}, bf16[1,128,1536]{2,1,0:T(8,128)(2,1)S(1)}) custom-call(bf16[8,1536]{1,0:T(8,128)(2,1)} %tokens_hbm.1, s32[2,8]{1,0:T(2,128)} %bitcast.3, bf16[8,6144]{1,0:T(8,128)(2,1)} %bitcast.2, bf16[1,6144,4096]{2,1,0:T(8,128)(2,1)} %up_hbm.1, bf16[1,4096,6144]{2,1,0:T(8,128)(2,1)} %down_hbm.1, ...), custom_call_target="tpu_custom_call" | custom-call | tf_op jit(solution)/shard_map/pallas_call | solution.py:433
  40.9 0.8 %shard_map.96 = (bf16[8,1536]{1,0:T(8,128)(2,1)}, bf16[1,128,1536]{2,1,0:T(8,128)(2,1)}) custom-call(bf16[8,1536]{1,0:T(8,128)(2,1)S(1)} %get-tuple-element.4.mixed, bf16[1,128,1536]{2,1,0:T(8,128)(2,1)S(1)} %get-tuple-element.5.attended), custom_call_target="tpu_custom_call" | custom-call | tf_op jit(solution)/shard_map/pallas_call | solution.py:472

commit v2 on v1

--- a/solution.py
+++ b/solution.py
@@ -51,6 +51,7 @@
     small_sem,
     up_sem,
     down_sem,
+    own_sem,
     send_sem,
     plane_sem,
     y_sem,
@@ -59,15 +60,14 @@
     term_sem,
     back_sem,
 ):
-    n_sec, n_dp, cols, experts, fold, up_group, rows = dims
+    n_sec, n_dp, cols, experts, fold, tail, pieces = dims
     per_block, width = tokens.shape
     ff = down_hbm.shape[1]
-    slots, wide, part = per_block // fold, width // fold, cols // fold
-    up_blocks, sec_blocks = ff // cols, width // cols
-    groups, freed = up_blocks // up_group, up_group * width // rows
-    down_units = ff // rows
+    slots, wide, part = per_block // fold, width // fold, tail // fold
+    ring_cols = ring.shape[1]
+    up_runs, sec_blocks = ff // ring_cols, width // cols
     per_expert = n_dp // experts
-    away = (n_sec - 1) * sec_blocks
+    away, own = (n_sec - 1) * sec_blocks, width // tail
     bf16, f32 = jnp.bfloat16, jnp.float32
     s, g = lax.axis_index("section"), lax.axis_index("dp")
     half = n_sec // 2
@@ -91,17 +91,18 @@
     def section_of(j):
         return (y + half - j // 2) % half * 2 + (core + j) % 2
 
-    def up_copy(j, n):
-        unit = j * up_blocks + n
+    def up_copy(unit):
         return pltpu.make_async_copy(
-            up_hbm.at[0, aligned(section_of(j), width), aligned(n, cols)],
+            up_hbm.at[
+                0, aligned(section_of(unit // up_runs), width), aligned(unit % up_runs, ring_cols)
+            ],
             ring.at[aligned(unit, width)],
             up_sem.at[unit],
         )
 
-    @pl.loop(0, n_sec * up_blocks)
+    @pl.loop(0, n_sec * up_runs)
     def _(unit):
-        up_copy(unit // up_blocks, unit % up_blocks).start()
+        up_copy(unit).start()
 
     barrier = pltpu.get_barrier_semaphore()
 
@@ -218,13 +219,31 @@
         to_y, to_core = (y + 1 + turn // 2) % half, (core + 1 + turn) % 2
         return to_y * 2 + to_core, block % sec_blocks
 
-    def down_copy(unit):
-        block, piece = unit // down_units, unit % down_units
+    def ring_at(index, size):
+        return ring.at[aligned(index * size // ring_cols, ff), aligned(index % (ring_cols // size), size)]
+
+    def down_copy(block):
         sec, col = down_place(block)
         return pltpu.make_async_copy(
-            down_hbm.at[0, aligned(piece, rows), aligned(sec * sec_blocks + col, cols)],
-            ring.at[aligned(unit, rows)],
+            down_hbm.at[0, :, aligned(sec * sec_blocks + col, cols)],
+            ring_at(block, cols),
             down_sem.at[block],
+        )
+
+    def own_at(index):
+        return ring_at(away * cols // tail + index, tail)
+
+    def own_copy(index):
+        return pltpu.make_async_copy(
+            down_hbm.at[0, :, aligned(s * own + index, tail)], own_at(index), own_sem.at[index]
+        )
+
+    def last_copy(piece):
+        rows = aligned(piece, ff // pieces)
+        return pltpu.make_async_copy(
+            down_hbm.at[0, rows, aligned(s * own + own - 1, tail)],
+            own_at(own - 1).at[rows],
+            own_sem.at[own - 1 + piece],
         )
 
     low = iota((per_block, 1), 0) < slots
@@ -252,16 +271,13 @@
     def phase(j, first, last):
         assemble(j, section_of(j))
 
-        @pl.loop(0, groups)
-        def _(group):
-            for lane in range(up_group):
-                up_copy(j, group * up_group + lane).wait()
-            for lane in range(up_group):
-                n = group * up_group + lane
-                at = aligned(n, cols)
+        for unit in range(j * up_runs, (j + 1) * up_runs):
+            up_copy(unit).wait()
+            for lane in range(ring_cols // cols):
+                at = pl.ds(unit % up_runs * ring_cols + lane * cols, cols)
                 value = jnp.dot(
                     x_rows[j],
-                    ring[aligned(j * up_blocks + n, width), :],
+                    ring[unit * width : (unit + 1) * width, lane * cols : (lane + 1) * cols],
                     preferred_element_type=f32,
                 )
                 if not first:
@@ -270,10 +286,23 @@
                     hidden[:, at] = (value / (1.0 + jnp.exp(-value))).astype(bf16)
                 else:
                     acc[:, at] = value
-
-            @pl.loop(0, freed)
-            def _(unit):
-                down_copy((j * groups + group) * freed + unit).start()
+            start_down(unit)
+
+    def start_down(unit):
+        begin, end = (edge * width // ff * ring_cols for edge in (unit, unit + 1))
+        bound = away * cols
+
+        @pl.loop(min(begin, bound) // cols, min(end, bound) // cols)
+        def _(block):
+            down_copy(block).start()
+
+        @pl.loop(max(begin - bound, 0) // tail, min(max(end - bound, 0) // tail, own - 1))
+        def _(index):
+            own_copy(index).start()
+
+        if unit == n_sec * up_runs - 1:
+            for piece in range(pieces):
+                last_copy(piece).start()
 
     await_bytes(planes.at[s, pl.ds(0, n_dp - 1)], plane_sem)
 
@@ -289,23 +318,15 @@
     send(planes.at[s], planes.at[s], (send_sem.at[1], pair_sem.at[0]), partner)
     phase(0, True, False)
 
-    @pl.loop(1, n_sec - 1)
-    def _(j):
+    for j in range(1, n_sec):
         sec, t = section_of(j), j // 2
-
-        @pl.when(j % 2 == 0)
-        def _():
+        if j % 2 == 0:
             await_bytes(planes.at[sec], y_sem.at[t])
             send(planes.at[sec], planes.at[sec], (send_sem.at[1], pair_sem.at[t]), partner)
-
-        @pl.when(j % 2 == 1)
-        def _():
+        else:
             await_bytes(planes.at[sec], pair_sem.at[t])
-
-        phase(j, False, False)
-
-    await_bytes(planes.at[section_of(n_sec - 1)], pair_sem.at[half - 1])
-    phase(n_sec - 1, False, True)
+        phase(j, False, j == n_sec - 1)
+
     attend(2)
 
     await_bytes(logit_terms.at[pl.ds(0, n_sec - 1)], logit_sem)
@@ -340,7 +361,7 @@
     coefficient[...] = jnp.concatenate([coarse, weights - coarse], axis=0).astype(bf16)
 
     def down_block(block):
-        taken = ring.at[aligned(block, ff)]
+        taken = ring_at(block, cols)
         await_bytes(taken, down_sem.at[block])
         return jnp.dot(hidden[...], taken[...], preferred_element_type=f32)
 
@@ -357,11 +378,13 @@
 
     await_bytes(terms, term_sem)
 
-    @pl.loop(0, sec_blocks)
-    def _(block):
-        summed = down_block(away + block)
-        for term in range(n_sec - 1):
-            summed += terms[term, :, aligned(block, cols)].astype(f32)
+    def peers_terms(index):
+        summed = terms[0, :, aligned(index, tail)].astype(f32)
+        for term in range(1, n_sec - 1):
+            summed += terms[term, :, aligned(index, tail)].astype(f32)
+        return summed
+
+    def give_back(index, summed):
         for b in range(n_dp // fold):
             piece = summed[b * per_block : (b + 1) * per_block]
             if fold == 2:
@@ -369,32 +392,48 @@
             else:
                 back = [piece]
             for i in range(fold):
-                returning[block, b * fold + i] = back[i].astype(bf16)
+                returning[index, b * fold + i] = back[i].astype(bf16)
 
         @pl.loop(1, n_dp)
         def _(offset):
             b = (g + offset) % n_dp
             send(
-                returning.at[block, b],
-                received.at[block, g],
-                (send_sem.at[4], back_sem.at[block]),
+                returning.at[index, b],
+                received.at[index, g],
+                (send_sem.at[4], back_sem.at[index]),
                 {"section": s, "dp": b},
             )
 
-        received[block, g] = returning[block, g]
-
-    @pl.loop(0, sec_blocks)
-    def _(block):
-        await_bytes(received.at[block, pl.ds(0, n_dp - 1)], back_sem.at[block])
+        received[index, g] = returning[index, g]
+
+    @pl.loop(0, own - 1)
+    def _(index):
+        taken = own_at(index)
+        await_bytes(taken, own_sem.at[index])
+        value = jnp.dot(hidden[...], taken[...], preferred_element_type=f32)
+        give_back(index, value + peers_terms(index))
+
+    summed = peers_terms(own - 1)
+    for piece in range(pieces):
+        rows = pl.ds(piece * (ff // pieces), ff // pieces)
+        taken = own_at(own - 1).at[rows]
+        await_bytes(taken, own_sem.at[own - 1 + piece])
+        summed += jnp.dot(hidden[:, rows], taken[...], preferred_element_type=f32)
+    give_back(own - 1, summed)
+
+    @pl.loop(0, own)
+    def _(index):
+        await_bytes(received.at[index, pl.ds(0, n_dp - 1)], back_sem.at[index])
         rows_back = jnp.concatenate(
-            [received[block, b].astype(f32) for b in range(n_dp)], axis=0
+            [received[index, b].astype(f32) for b in range(n_dp)], axis=0
         ).astype(bf16)
         both = jnp.dot(coefficient[...], rows_back, preferred_element_type=f32)
         tall = fold * per_block
         total = both[:tall] + both[tall:]
         for h in range(fold):
-            at = pl.ds(pl.multiple_of(block * cols + h * part, part), part)
-            mixed[:, at] = total[h * per_block : (h + 1) * per_block].astype(bf16)
+            mixed[:, aligned(index * fold + h, part)] = total[
+                h * per_block : (h + 1) * per_block
+            ].astype(bf16)
 
     await_bytes(planes.at[0, pl.ds(0, n_dp - 1)], send_sem.at[0])
     await_bytes(planes.at[pl.ds(0, n_sec - 1)], send_sem.at[1])
@@ -421,32 +460,33 @@
     ff = w_up.shape[2]
     length = attn_queries.shape[1]
     cols = math.gcd(ff, width)
-    fold = per_block // CAP if cols % (2 * LANES) == 0 else 1
-    up_group = math.gcd(ff // cols, 4)
-    rows = math.gcd(up_group * width, ff)
-    slots, wide, part = per_block // fold, width // fold, cols // fold
-    tall, down_blocks, sec_blocks = n_dp * slots, model // cols, width // cols
+    ring_cols = math.gcd(ff, model)
+    fold, tail = per_block // CAP if cols % (2 * LANES) == 0 else 1, cols
+    pieces = math.gcd(ff // (2 * LANES), 4) if ff % (2 * LANES) == 0 else 1
+    slots, wide, part, own = per_block // fold, width // fold, tail // fold, width // tail
+    tall, sec_blocks = n_dp * slots, width // cols
+    away = (n_sec - 1) * sec_blocks
     bf16, f32 = jnp.bfloat16, jnp.float32
     any_spec = pl.BlockSpec(memory_space=pl.ANY)
     vmem_spec = pl.BlockSpec(memory_space=pltpu.VMEM)
     shapes = tokens.shape, attn_queries.shape
     held = pl.pallas_call(
-        functools.partial(kernel, (n_sec, n_dp, cols, experts, fold, up_group, rows)),
+        functools.partial(kernel, (n_sec, n_dp, cols, experts, fold, tail, pieces)),
         out_shape=tuple(pltpu.VMEM(shape, bf16) for shape in shapes),
         in_specs=[any_spec] * 8,
         out_specs=(vmem_spec, vmem_spec),
         scratch_shapes=[
-            pltpu.VMEM((model * ff // cols, cols), bf16),
+            pltpu.VMEM((model * ff // ring_cols, ring_cols), bf16),
             pltpu.VMEM((per_block, width), bf16),
             pltpu.VMEM((experts, per_block, wide), bf16),
             pltpu.VMEM((n_sec, n_dp, per_block, wide), bf16),
             pltpu.VMEM((n_sec, tall, width), bf16),
             pltpu.VMEM((tall, ff), f32),
             pltpu.VMEM((tall, ff), bf16),
-            pltpu.VMEM((down_blocks - sec_blocks, tall, cols), bf16),
+            pltpu.VMEM((away, tall, cols), bf16),
             pltpu.VMEM((n_sec - 1, tall, width), bf16),
-            pltpu.VMEM((sec_blocks, n_dp, per_block, part), bf16),
-            pltpu.VMEM((sec_blocks, n_dp, per_block, part), bf16),
+            pltpu.VMEM((own, n_dp, per_block, part), bf16),
+            pltpu.VMEM((own, n_dp, per_block, part), bf16),
             pltpu.VMEM((experts, width), bf16),
             pltpu.VMEM((2, per_block), jnp.int32),
             pltpu.VMEM((n_sec, per_block, LANES), f32),
@@ -455,15 +495,16 @@
             pltpu.VMEM((length, width), bf16),
             pltpu.VMEM((length, width), bf16),
             pltpu.SemaphoreType.DMA((6,)),
-            pltpu.SemaphoreType.DMA((n_sec * ff // cols,)),
-            pltpu.SemaphoreType.DMA((down_blocks,)),
+            pltpu.SemaphoreType.DMA((n_sec * ff // ring_cols,)),
+            pltpu.SemaphoreType.DMA((away,)),
+            pltpu.SemaphoreType.DMA((own - 1 + pieces,)),
             pltpu.SemaphoreType.DMA((5,)),
             pltpu.SemaphoreType.DMA,
             pltpu.SemaphoreType.DMA((n_sec // 2,)),
             pltpu.SemaphoreType.DMA((n_sec // 2,)),
             pltpu.SemaphoreType.DMA,
             pltpu.SemaphoreType.DMA,
-            pltpu.SemaphoreType.DMA((sec_blocks,)),
+            pltpu.SemaphoreType.DMA((own,)),
         ],
         compiler_params=pltpu.CompilerParams(
             collective_id=0, has_side_effects=True, vmem_limit_bytes=62 * 2**20

time: 41.8 us -> 40.9 us (0.978)
  Pallas kernels: 41 us -> 40.1 us
    pallas_call x1, Pallas kernels: 40.3 us -> 39.4 us  [per_device(): pl.pallas_call(functools.partial(kernel, (n_sec, n_dp, cols, experts, fol...]
where the time goes in v2:
time: 40.9 us; the launch traced here: 40.8 us
  Pallas kernels  40.1 us (98%)
  between operations  0.64 us (2%)
    pallas_call x1, Pallas kernels, per_device(): pl.pallas_call(functools.partial(kernel, (n_sec, n_dp, cols, experts, fol...  39.4 us

profile of v2, /device:TPU:0, one launch (start us, length us, event | category | flops | bytes accessed | tf_op | source)
XLA Modules:
  0.0 40.8 jit_solution(14709923814205754846)
XLA Ops:
  0.6 39.4 %shard_map.95 = (bf16[8,1536]{1,0:T(8,128)(2,1)S(1)}, bf16[1,128,1536]{2,1,0:T(8,128)(2,1)S(1)}) custom-call(bf16[8,1536]{1,0:T(8,128)(2,1)} %tokens_hbm.1, s32[2,8]{1,0:T(2,128)} %bitcast.3, bf16[8,6144]{1,0:T(8,128)(2,1)} %bitcast.2, bf16[1,6144,4096]{2,1,0:T(8,128)(2,1)} %up_hbm.1, bf16[1,4096,6144]{2,1,0:T(8,128)(2,1)} %down_hbm.1, ...), custom_call_target="tpu_custom_call" | custom-call | tf_op jit(solution)/shard_map/pallas_call | solution.py:473
  40.0 0.8 %shard_map.96 = (bf16[8,1536]{1,0:T(8,128)(2,1)}, bf16[1,128,1536]{2,1,0:T(8,128)(2,1)}) custom-call(bf16[8,1536]{1,0:T(8,128)(2,1)S(1)} %get-tuple-element.4.mixed, bf16[1,128,1536]{2,1,0:T(8,128)(2,1)S(1)} %get-tuple-element.5.attended), custom_call_target="tpu_custom_call" | custom-call | tf_op jit(solution)/shard_map/pallas_call | solution.py:513

commit v3 on v2

--- a/solution.py
+++ b/solution.py
@@ -233,17 +233,12 @@
     def own_at(index):
         return ring_at(away * cols // tail + index, tail)
 
-    def own_copy(index):
-        return pltpu.make_async_copy(
-            down_hbm.at[0, :, aligned(s * own + index, tail)], own_at(index), own_sem.at[index]
-        )
-
-    def last_copy(piece):
+    def own_copy(index, piece):
         rows = aligned(piece, ff // pieces)
         return pltpu.make_async_copy(
-            down_hbm.at[0, rows, aligned(s * own + own - 1, tail)],
-            own_at(own - 1).at[rows],
-            own_sem.at[own - 1 + piece],
+            down_hbm.at[0, rows, aligned(s * own + index, tail)],
+            own_at(index).at[rows],
+            own_sem.at[index * pieces + piece],
         )
 
     low = iota((per_block, 1), 0) < slots
@@ -296,13 +291,10 @@
         def _(block):
             down_copy(block).start()
 
-        @pl.loop(max(begin - bound, 0) // tail, min(max(end - bound, 0) // tail, own - 1))
+        @pl.loop(max(begin - bound, 0) // tail, max(end - bound, 0) // tail)
         def _(index):
-            own_copy(index).start()
-
-        if unit == n_sec * up_runs - 1:
             for piece in range(pieces):
-                last_copy(piece).start()
+                own_copy(index, piece).start()
 
     await_bytes(planes.at[s, pl.ds(0, n_dp - 1)], plane_sem)
 
@@ -406,20 +398,15 @@
 
         received[index, g] = returning[index, g]
 
-    @pl.loop(0, own - 1)
+    @pl.loop(0, own)
     def _(index):
-        taken = own_at(index)
-        await_bytes(taken, own_sem.at[index])
-        value = jnp.dot(hidden[...], taken[...], preferred_element_type=f32)
-        give_back(index, value + peers_terms(index))
-
-    summed = peers_terms(own - 1)
-    for piece in range(pieces):
-        rows = pl.ds(piece * (ff // pieces), ff // pieces)
-        taken = own_at(own - 1).at[rows]
-        await_bytes(taken, own_sem.at[own - 1 + piece])
-        summed += jnp.dot(hidden[:, rows], taken[...], preferred_element_type=f32)
-    give_back(own - 1, summed)
+        summed = peers_terms(index)
+        for piece in range(pieces):
+            rows = pl.ds(piece * (ff // pieces), ff // pieces)
+            taken = own_at(index).at[rows]
+            await_bytes(taken, own_sem.at[index * pieces + piece])
+            summed += jnp.dot(hidden[:, rows], taken[...], preferred_element_type=f32)
+        give_back(index, summed)
 
     @pl.loop(0, own)
     def _(index):
@@ -462,7 +449,7 @@
     cols = math.gcd(ff, width)
     ring_cols = math.gcd(ff, model)
     fold, tail = per_block // CAP if cols % (2 * LANES) == 0 else 1, cols
-    pieces = math.gcd(ff // (2 * LANES), 4) if ff % (2 * LANES) == 0 else 1
+    pieces = math.gcd(ff // (2 * LANES), 2) if ff % (2 * LANES) == 0 else 1
     slots, wide, part, own = per_block // fold, width // fold, tail // fold, width // tail
     tall, sec_blocks = n_dp * slots, width // cols
     away = (n_sec - 1) * sec_blocks
@@ -497,7 +484,7 @@
             pltpu.SemaphoreType.DMA((6,)),
             pltpu.SemaphoreType.DMA((n_sec * ff // ring_cols,)),
             pltpu.SemaphoreType.DMA((away,)),
-            pltpu.SemaphoreType.DMA((own - 1 + pieces,)),
+            pltpu.SemaphoreType.DMA((own * pieces,)),
             pltpu.SemaphoreType.DMA((5,)),
             pltpu.SemaphoreType.DMA,
             pltpu.SemaphoreType.DMA((n_sec // 2,)),

time: 40.9 us -> 40.7 us (level)
  no operation moved by 1% of the time
where the time goes in v3:
time: 40.7 us; the launch traced here: 40.5 us
  Pallas kernels  39.9 us (98%)
  between operations  0.64 us (2%)
    pallas_call x1, Pallas kernels, per_device(): pl.pallas_call(functools.partial(kernel, (n_sec, n_dp, cols, experts, fol...  39.1 us

profile of v3, /device:TPU:0, one launch (start us, length us, event | category | flops | bytes accessed | tf_op | source)
XLA Modules:
  0.0 40.5 jit_solution(14054519445429822280)
XLA Ops:
  0.6 39.1 %shard_map.95 = (bf16[8,1536]{1,0:T(8,128)(2,1)S(1)}, bf16[1,128,1536]{2,1,0:T(8,128)(2,1)S(1)}) custom-call(bf16[8,1536]{1,0:T(8,128)(2,1)} %tokens_hbm.1, s32[2,8]{1,0:T(2,128)} %bitcast.3, bf16[8,6144]{1,0:T(8,128)(2,1)} %bitcast.2, bf16[1,6144,4096]{2,1,0:T(8,128)(2,1)} %up_hbm.1, bf16[1,4096,6144]{2,1,0:T(8,128)(2,1)} %down_hbm.1, ...), custom_call_target="tpu_custom_call" | custom-call | tf_op jit(solution)/shard_map/pallas_call | solution.py:460
  39.8 0.8 %shard_map.96 = (bf16[8,1536]{1,0:T(8,128)(2,1)}, bf16[1,128,1536]{2,1,0:T(8,128)(2,1)}) custom-call(bf16[8,1536]{1,0:T(8,128)(2,1)S(1)} %get-tuple-element.4.mixed, bf16[1,128,1536]{2,1,0:T(8,128)(2,1)S(1)} %get-tuple-element.5.attended), custom_call_target="tpu_custom_call" | custom-call | tf_op jit(solution)/shard_map/pallas_call | solution.py:500
